TPU v7x, 128 devices: a whole 4x4x4 slice. The times are simulated.
128 devices in a mesh: wide: 32 (over z, y, x_hi), narrow: 4 (over x_lo, core).
Axes of the slice: x: 4 (x_hi: 2, x_lo: 2; x = x_hi * 2 + x_lo), y: 4, z: 4, core: 2. Of those that a mesh axis runs over, the one named last changes fastest.
Arguments:
- values: float32 [512, 65536], P(('wide', 'narrow')), may hold values from -200 to 200, as said below
- cloud_words: int32 [512, 2048], P(('wide', 'narrow')), may hold values from -2147483648 to 2147483647, as said below
- history_len: int32 [1], replicated, may hold values from 96 to 256
- monitor_start: int32 [1], replicated, may hold values from 256 to 384
- boundary_table: int32 [512], replicated, may hold values from 500 to 2000
Outputs:
- ratio: float32 [512, 65536], P(('wide', 'narrow'))
- peak_so_far: float32 [512, 65536], P(('wide', 'narrow'))
Inputs may be any that keep to these rules, and one draw needn't show every extreme that they name: `values`: values of an index series, mixed noise and a seasonal cycle of varying scale. `cloud_words`: bit b of word j in the row of date t is 1 when pixel 32 j + b is clear at date t; the first 16 dates are clear for every pixel.
All inputs are finite; a program needn't handle non-finite values.
Results may differ from a plain program's by a relative error of at most 0.0003.
Values sent between devices are 32-bit elements; how exact they have to be, the bound alone decides.
A program may use at most 64 MiB of HBM per device.

v0:
```python
import math

import jax
import jax.numpy as jnp
from jax import lax
from jax.sharding import PartitionSpec as P

PERIOD = 46
HARMONICS = 3
COLS = 8
WINDOW = 64


HIGH = lax.Precision.HIGHEST


def unpack_clear(words):
    shifts = jnp.arange(32, dtype=jnp.int32)
    flags = jnp.bitwise_and(jnp.right_shift(words[:, :, None], shifts[None, None, :]), jnp.int32(1))
    return flags.reshape(words.shape[0], words.shape[1] * 32).astype(jnp.float32)


def harmonic_design(dates):
    day_float = jnp.arange(dates, dtype=jnp.int32).astype(jnp.float32)
    columns = [jnp.ones((dates,), jnp.float32), day_float / dates]
    for harmonic in range(1, HARMONICS + 1):
        phases = 2.0 * math.pi * harmonic / PERIOD * day_float
        columns.append(jnp.cos(phases))
        columns.append(jnp.sin(phases))
    return jnp.stack(columns, axis=1)


def solve_batched(normal_mat, target):
    size_cols = normal_mat.shape[0]
    factor = [[None] * size_cols for row_idx in range(size_cols)]
    for row_idx in range(size_cols):
        for col_idx in range(row_idx + 1):
            summed = normal_mat[row_idx, col_idx]
            for mid_idx in range(col_idx):
                summed = summed - factor[row_idx][mid_idx] * factor[col_idx][mid_idx]
            if row_idx == col_idx:
                factor[row_idx][col_idx] = jnp.sqrt(summed)
            else:
                factor[row_idx][col_idx] = summed / factor[col_idx][col_idx]
    forward = []
    for row_idx in range(size_cols):
        summed = target[row_idx]
        for mid_idx in range(row_idx):
            summed = summed - factor[row_idx][mid_idx] * forward[mid_idx]
        forward.append(summed / factor[row_idx][row_idx])
    solution = [None] * size_cols
    for row_idx in reversed(range(size_cols)):
        summed = forward[row_idx]
        for mid_idx in range(row_idx + 1, size_cols):
            summed = summed - factor[mid_idx][row_idx] * solution[mid_idx]
        solution[row_idx] = summed / factor[row_idx][row_idx]
    return jnp.stack(solution, axis=0)


def fit_statistic(values, clear, history_len, monitor_start, boundary_table):
    dates = values.shape[0]
    day = jnp.arange(dates, dtype=jnp.int32)
    design = harmonic_design(dates)
    in_history = (day < history_len[0]).astype(jnp.float32)[:, None]
    weight = clear * in_history
    outer = (design[:, :, None] * design[:, None, :]).reshape(dates, COLS * COLS)
    normal_mat = jnp.dot(
        outer.T, weight, precision=HIGH, preferred_element_type=jnp.float32
    ).reshape(COLS, COLS, -1)
    target = jnp.dot(design.T, weight * values, precision=HIGH, preferred_element_type=jnp.float32)
    coeffs = solve_batched(normal_mat, target)
    fitted = jnp.dot(design, coeffs, precision=HIGH, preferred_element_type=jnp.float32)
    resid = clear * (values - fitted)
    count = jnp.sum(weight, axis=0)
    squares = jnp.sum(weight * resid * resid, axis=0)
    sigma = jnp.sqrt(squares / (count - COLS) + 1e-06)
    lagged = day[:, None] - day[None, :]
    banded = ((lagged >= 0) & (lagged < WINDOW)).astype(jnp.float32)
    moving = jnp.dot(banded, resid, precision=HIGH, preferred_element_type=jnp.float32)
    scaled = moving / (sigma * jnp.sqrt(count))[None, :]
    bounds = boundary_table.astype(jnp.float32) * 0.001
    watching = (day >= monitor_start[0])[:, None]
    return jnp.where(watching, scaled / bounds[:, None], jnp.float32(0.0))


def per_device(values, cloud_words, history_len, monitor_start, boundary_table):
    arrived = lax.all_to_all(values, ("wide", "narrow"), split_axis=1, concat_axis=0, tiled=True)
    words = lax.all_to_all(cloud_words, ("wide", "narrow"), split_axis=1, concat_axis=0, tiled=True)
    ratio = fit_statistic(arrived, unpack_clear(words), history_len, monitor_start, boundary_table)
    outgoing = jnp.stack([ratio, lax.cummax(jnp.abs(ratio), axis=0)])
    returned = lax.all_to_all(outgoing, ("wide", "narrow"), split_axis=1, concat_axis=2, tiled=True)
    date_ratio = returned[0]
    peak = returned[1]
    return (date_ratio, peak)


def solution(mesh):
    placed = (P(("wide", "narrow"), None), P(("wide", "narrow"), None), P(), P(), P())
    return jax.shard_map(
        per_device,
        mesh=mesh,
        in_specs=placed,
        out_specs=(P(("wide", "narrow"), None), P(("wide", "narrow"), None)),
        check_vma=False,
    )
```

profile of v0, /device:TPU:1, one launch (start us, length us, event | category | flops | bytes accessed | tf_op | source)
XLA Modules:
  0.0 98.5 jit_solution(789986749912056951)
XLA Ops:
  0.6 0.9 all_to_all.37
  1.5 0.9 copy.33
  2.4 11.5 %all-to-all-start = ((s32[4,128,16]{2,0,1:T(4,128)}), s32[4,128,16]{2,0,1:T(4,128)S(1)}, u32[]{:S(2)}, u32[]{:S(2)}) async-start(s32[4,128,16]{2,0,1:T(4,128)} %copy.33), calls=%async_computation | async-start | bytes 524288 | tf_op jit(solution)/shard_map/all_to_all | solution.py:88
  13.9 0.1 fusion.104
  14.0 0.1 fusion.102
  14.1 0.1 fusion.100
  14.2 0.1 convert_multiply_fusion.7
  15.6 0.7 convert_multiply_fusion.3
  16.3 0.1 shift_right_arithmetic.38
  16.4 8.5 %all-to-all-done = s32[4,128,16]{2,0,1:T(4,128)S(1)} async-done(((s32[4,128,16]{2,0,1:T(4,128)}), s32[4,128,16]{2,0,1:T(4,128)S(1)}, u32[]{:S(2)}, u32[]{:S(2)}) %all-to-all-start) | async-done | bytes 32800 | tf_op jit(solution)/shard_map/all_to_all | solution.py:88
  25.0 4.4 %all-to-all-start.1 = ((f32[4,128,512]{2,0,1:T(4,128)}), f32[4,128,512]{2,0,1:T(4,128)S(1)}, u32[]{:S(2)}, u32[]{:S(2)}) async-start(f32[4,128,512]{2,0,1:T(4,128)} %bitcast.453), calls=%async_computation.1 | async-start | bytes 2097152 | tf_op jit(solution)/shard_map/all_to_all | solution.py:87
  29.4 0.1 copy.34
  29.5 0.3 fusion.19
  29.8 1.1 %shift_right_arithmetic.35 = s32[512,16,32]{0,2,1:T(8,128)} broadcast(s32[512,16]{0,1:T(8,128)S(1)} %copy.34), dimensions={0,1} | broadcast | bytes 1081344 | tf_op jit(solution)/shard_map/shift_right_arithmetic | solution.py:19
  30.9 1.6 %copy.35 = s32[512,512]{1,0:T(8,128)S(1)} copy(s32[512,512]{0,1:T(8,128)} %bitcast.450) | data formatting | bytes 2097152 | tf_op jit(solution)/shard_map/shift_right_arithmetic | solution.py:19
  32.4 0.1 sub.3613
  32.5 0.1 sqrt.482
  32.6 1.1 %fusion.20 = f32[8,8,512]{2,1,0:T(8,128)S(1)} fusion(f32[512,512,1]{0,1,2:T(8,128)S(1)} %bitcast.448, f32[512,8]{0,1:T(8,128)S(1)} %stack.10), kind=kOutput, calls=%fused_computation.31 | convolution fusion | flops 201359360 | bytes 1196032 | tf_op jit(solution)/shard_map/dot_general | solution.py:67
  33.8 14.8 %all-to-all-done.1 = f32[4,128,512]{2,0,1:T(4,128)S(1)} async-done(((f32[4,128,512]{2,0,1:T(4,128)}), f32[4,128,512]{2,0,1:T(4,128)S(1)}, u32[]{:S(2)}, u32[]{:S(2)}) %all-to-all-start.1) | async-done | bytes 1048608 | tf_op jit(solution)/shard_map/all_to_all | solution.py:87
  48.6 0.4 all_to_all.43
  49.0 0.8 fusion.6
  49.8 0.2 subtract_divide_fusion.6
  50.0 0.1 rsqrt_multiply_fusion
  50.1 0.2 bitcast_divide_fusion.1
  50.3 1.3 %fusion.1 = (f32[512]{0:T(512)S(1)}, f32[512,512]{1,0:T(8,128)S(1)}) fusion(s32[512,512]{1,0:T(8,128)S(1)} %copy.35, f32[512]{0:T(512)S(1)} %fusion.105, s32[512]{0:T(512)S(1)} %shift_right_arithmetic.38, f32[512,512]{1,0:T(8,128)S(1)} %all_to_all.43, f32[512,8]{0,1:T(8,128)S(1)} %stack.10, f32[8,512]{1,0:T(8,128)S(1)} %stack.11), kind=kOutput, calls=%fused_computation.4 | convolution fusion | flops 27524608 | bytes 3184640 | tf_op jit(solution)/shard_map/dot_general | solution.py:72
  51.6 1.1 %fusion.11 = f32[512,512]{1,0:T(8,128)S(1)} fusion(f32[512,512]{1,0:T(8,128)S(1)} %get-tuple-element.89), kind=kOutput, calls=%fused_computation.23 | convolution fusion | flops 1611661312 | bytes 2097152 | tf_op jit(solution)/shard_map/dot_general | solution.py:79
  52.7 0.3 copy.38
  53.0 0.4 select_bitcast_fusion
  53.5 0.7 fusion.4
  54.2 0.1 broadcast_maximum_fusion
  54.3 0.6 copy.40
  54.9 0.1 copy.54
  55.0 0.2 pad_maximum_fusion
  55.2 2.5 %copy.41 = f32[2,512,512]{2,0,1:T(2,128)} copy(f32[2,512,512]{1,2,0:T(8,128)S(1)} %pad_maximum_fusion) | data formatting | bytes 4194304 | tf_op jit(solution)/shard_map/stack | solution.py:90
  57.7 35.2 %all_to_all.50 = f32[2,512,512]{2,0,1:T(2,128)S(1)} all-to-all(f32[2,512,512]{2,0,1:T(2,128)} %copy.41), channel_id=1, replica_groups=mesh['wide'=32,'narrow'=4] {'wide','narrow'}, dimensions={1} | all-to-all | bytes 4194304 | tf_op jit(solution)/shard_map/all_to_all | solution.py:91
  92.9 1.6 %fusion.131 = (f32[1,4,128,512]{3,0,1,2:T(1,128)S(1)}, f32[1,4,128,512]{3,0,1,2:T(1,128)S(1)}) fusion(f32[2,4,128,512]{3,0,1,2:T(2,128)S(1)} %bitcast.444), kind=kLoop, calls=%fused_computation.252 | loop fusion | bytes 4194304 | tf_op jit(solution)/shard_map/slice | solution.py:93
  94.5 0.3 copy.55
  94.9 1.6 %copy.48 = f32[1,4,128,512]{3,1,2,0:T(4,128)} copy(f32[1,4,128,512]{3,2,1,0:T(8,128)S(1)} %copy.55) | data formatting | bytes 2097152
  96.5 0.3 copy.56
  96.9 1.6 %copy.47 = f32[1,4,128,512]{3,1,2,0:T(4,128)} copy(f32[1,4,128,512]{3,2,1,0:T(8,128)S(1)} %copy.56) | data formatting | bytes 2097152
  (15 shorter events, 0.3 us)
Async XLA Ops:
  2.4 22.6 %all-to-all-start = ((s32[4,128,16]{2,0,1:T(4,128)}), s32[4,128,16]{2,0,1:T(4,128)S(1)}, u32[]{:S(2)}, u32[]{:S(2)}) async-start(s32[4,128,16]{2,0,1:T(4,128)} %copy.33), calls=%async_computation | async-start | bytes 524288 | tf_op jit(solution)/shard_map/all_to_all | solution.py:88
  25.0 23.7 %all-to-all-start.1 = ((f32[4,128,512]{2,0,1:T(4,128)}), f32[4,128,512]{2,0,1:T(4,128)S(1)}, u32[]{:S(2)}, u32[]{:S(2)}) async-start(f32[4,128,512]{2,0,1:T(4,128)} %bitcast.453), calls=%async_computation.1 | async-start | bytes 2097152 | tf_op jit(solution)/shard_map/all_to_all | solution.py:87
where the time goes:
time: 98.9 us; the launch traced here: 98.5 us
  blocking collectives  35.2 us (36%)
  waiting for transfers between devices  23.3 us (24%)
  starting transfers between devices  15.9 us (16%)
  local copies, waits for them, and re-layouts  14.2 us (14%)
  matrix products  4.28 us (4%)
  other arithmetic  3.39 us (3%)
  between operations  2.14 us (2%)
    all_to_all x1, blocking collectives, per_device(): lax.all_to_all(outgoing, ('wide', 'narrow'), split_axis=1, concat_axis=2,...  35.2 us
    all_to_all x1, waiting for transfers between devices, per_device(): lax.all_to_all(values, ('wide', 'narrow'), split_axis=1, concat_axis=0, t...  14.8 us
    all_to_all x1, starting transfers between devices, per_device(): lax.all_to_all(cloud_words, ('wide', 'narrow'), split_axis=1, concat_axis...  11.5 us
    all_to_all x1, waiting for transfers between devices, per_device(): lax.all_to_all(cloud_words, ('wide', 'narrow'), split_axis=1, concat_axis...  8.52 us
    all_to_all x1, starting transfers between devices, per_device(): lax.all_to_all(values, ('wide', 'narrow'), split_axis=1, concat_axis=0, t...  4.42 us
    unnamed x4, local copies, waits for them, and re-layouts  3.37 us
    another operation x2, local copies, waits for them, and re-layouts, per_device(): outgoing = jnp.stack([ratio, lax.cummax(jnp.abs(ratio), axis=0)])  3.04 us
    shift_right_arithmetic x5, local copies, waits for them, and re-layouts, unpack_clear(): jnp.right_shift(words[:, :, None], shifts[None, None, :])  2.83 us
  transfers between devices with their start and end apart: 2, of which 2 were waited for; matrix products, arithmetic and copies ran while one was open for 6% of the time, Pallas kernels for 0%

commit v1 on v0

v1 whole, which is shorter than its diff:
```python
import math
import random

import jax
import jax.numpy as jnp
import ml_dtypes
import numpy as np
from jax import lax
from jax.experimental import pallas as pl
from jax.experimental.pallas import tpu as pltpu
from jax.sharding import PartitionSpec as P

PERIOD = 46
HARMONICS = 3
COLS = 8
WINDOW = 64
DATES = 512
NDEV = 128
MESH = pl.DeviceIdType.MESH
ANY = pl.BlockSpec(memory_space=pl.ANY)


def pieces(array, count=3):
    out = []
    rest = array.astype(np.float64)
    for _ in range(count):
        part = rest.astype(np.float32).astype(ml_dtypes.bfloat16)
        out.append(part)
        rest = rest - part.astype(np.float64)
    return out


def constants():
    day = np.arange(DATES, dtype=np.float32)
    columns = [np.ones((DATES,), np.float32), day / np.float32(DATES)]
    for harmonic in range(1, HARMONICS + 1):
        phases = np.float32(2.0 * math.pi * harmonic / PERIOD) * day
        columns.append(np.cos(phases.astype(np.float64)).astype(np.float32))
        columns.append(np.sin(phases.astype(np.float64)).astype(np.float32))
    design = np.stack(columns, axis=1)
    row = np.arange(NDEV * 8)
    date = 4 * (row // 8) + row % 4
    parity = (row % 8) // 4
    sub = np.arange(8)
    hist = 512
    same = (sub[:, None] // 4 == parity[None, :hist]).astype(np.float64)
    outer = []
    for r in range(COLS):
        for c in range(r + 1):
            prod = (design[:, r] * design[:, c]).astype(np.float32)
            outer.append(same * prod[date[:hist]][None, :])
    lhs_n = np.stack(pieces(np.concatenate(outer, axis=0)), axis=0)
    lhs_t = np.concatenate([same * design[date[:hist], c][None, :] for c in range(COLS)], axis=0)
    lhs_t = lhs_t.astype(np.float32)
    d_hi, d_mid, d_lo = [p.astype(np.float64) for p in pieces(design)]
    fit = np.zeros((NDEV * 8, 128))
    for c in range(COLS):
        for p in range(2):
            on = parity == p
            col = 8 * c + 4 * p
            for slot, part in enumerate((d_hi, d_hi, d_hi, d_mid)):
                fit[:, col + slot] = on * part[date, c]
            for slot, part in enumerate((d_lo, d_mid)):
                fit[:, 64 + col + slot] = on * part[date, c]
    fit = fit.astype(ml_dtypes.bfloat16)
    lag = (date[:128][:, None] + 64) - date[:256][None, :]
    band = (lag >= 0) & (lag < WINDOW) & (parity[:128][:, None] == parity[:256][None, :])
    band = band.astype(ml_dtypes.bfloat16)
    return lhs_n, lhs_t, fit, band


def order(count, seed):
    ranks = list(range(1, count))
    random.Random(seed).shuffle(ranks)
    return ranks


def device(index):
    return {"wide": lax.div(index, 4), "narrow": lax.rem(index, 4)}


def split3(x):
    hi = x.astype(jnp.bfloat16)
    rest = x - hi.astype(jnp.float32)
    mid = rest.astype(jnp.bfloat16)
    lo = (rest - mid.astype(jnp.float32)).astype(jnp.bfloat16)
    return hi, mid, lo


def both(ref, start, count):
    lower = ref[start : start + count, 0:8, :].reshape(count * 8, 128)
    upper = ref[start : start + count, 8:16, :].reshape(count * 8, 128)
    return jnp.concatenate([lower, upper], axis=1)


def factorise(lower):
    unit = [[None] * COLS for _ in range(COLS)]
    scaled = [[None] * COLS for _ in range(COLS)]
    inverse = []
    for col in range(COLS):
        for row in range(col, COLS):
            summed = lower[row][col]
            for mid in range(col):
                summed = summed - unit[row][mid] * scaled[col][mid]
            scaled[row][col] = summed
        inverse.append(1.0 / scaled[col][col])
        for row in range(col + 1, COLS):
            unit[row][col] = scaled[row][col] * inverse[col]
    return unit, inverse


def substitute(unit, inverse, target):
    forward = []
    for row in range(COLS):
        summed = target[row]
        for mid in range(row):
            summed = summed - unit[row][mid] * forward[mid]
        forward.append(summed)
    solved = [None] * COLS
    for row in reversed(range(COLS)):
        summed = forward[row] * inverse[row]
        for mid in range(row + 1, COLS):
            summed = summed - unit[mid][row] * solved[mid]
        solved[row] = summed
    return solved


def fit_kernel(
    hl_h, ms_h, bt_h, w_h, v_h, ln_h, lt_h, fm_h, bm_h, rb, eb,
    hl, ms, bt, wv, wmsg, wbuf, inb, clear, resid, ob, ebuf, ln, lt, fm, bm, invb, usave,
    csem, wsend, wrecv, vsend, vrecv, rsend, rrecv, esend, erecv,
):
    me = lax.axis_index("wide") * 4 + lax.axis_index("narrow")
    barrier = pltpu.get_barrier_semaphore()

    def greet(k, carry):
        other = lax.rem(me + k, NDEV)
        pl.semaphore_signal(barrier, inc=1, device_id=device(other), device_id_type=MESH)
        return carry

    lax.fori_loop(1, NDEV, greet, 0)
    loads = []
    for slot, (src, dst) in enumerate(
        ((w_h, wv), (hl_h, hl), (ms_h, ms), (bt_h, bt), (ln_h, ln), (lt_h, lt), (fm_h, fm), (bm_h, bm))
    ):
        loads.append(pltpu.make_async_copy(src, dst, csem.at[slot]))
        loads[-1].start()

    loads[0].wait()
    sub = lax.broadcasted_iota(jnp.int32, (8, 128), 0)
    lane = lax.broadcasted_iota(jnp.int32, (8, 128), 1)
    pick = 16 * sub + lax.rem(lane, 16)
    for tile in range(16):
        words = wv[:, 128 * tile : 128 * tile + 128]
        packed = jnp.zeros((8, 128), jnp.int32)
        for date in range(4):
            spread = jnp.broadcast_to(words[date : date + 1, :], (8, 128))
            taken = jnp.take_along_axis(spread, pick, axis=1)
            packed = jnp.where(lax.div(lane, 16) == date, taken, packed)
        wmsg[8 * tile : 8 * tile + 8] = packed.reshape(8, 1, 128)
    for load in loads[1:]:
        load.wait()
    for part in range(2):
        date = 256 + 128 * part + lax.broadcasted_iota(jnp.int32, (1, 128), 1)
        line = 1.0 / (bt[2 + part : 3 + part, :].astype(jnp.float32) * 0.001)
        line = jnp.where(date >= ms[0], line, 0.0)
        rows = lax.broadcasted_iota(jnp.int32, (256, 128), 0)
        lanes = lax.broadcasted_iota(jnp.int32, (256, 128), 1)
        own = 4 * lax.div(rows, 8) + lax.rem(rows, 4)
        column = jnp.sum(jnp.where(lanes == own, line, 0.0), axis=1, keepdims=True)
        invb[256 * part : 256 * part + 256, :] = jnp.broadcast_to(column, (256, 128))

    pl.semaphore_wait(barrier, NDEV - 1)

    wbuf[pl.ds(me, 1)] = wmsg[pl.ds(me, 1)]
    for step in order(NDEV, 1):
        other = lax.rem(me + step, NDEV)
        pltpu.make_async_remote_copy(
            wmsg.at[other], wbuf.at[me], wsend, wrecv, device_id=device(other), device_id_type=MESH
        ).start()
    pltpu.make_async_copy(v_h.at[me], inb.at[me], vrecv).start()
    for step in order(NDEV, 1):
        other = lax.rem(me + step, NDEV)
        pltpu.make_async_remote_copy(
            v_h.at[other], inb.at[me], vsend, vrecv, device_id=device(other), device_id_type=MESH
        ).start()

    rest = pl.ds(0, NDEV - 1)
    pltpu.make_async_copy(wmsg.at[rest], wbuf.at[rest], wrecv).wait()
    where_word = [16 * lax.rem(sub, 4) + 4 * (2 * half + lax.div(sub, 4)) + lax.div(lane, 32) for half in range(2)]
    bit = lax.rem(lane, 32)

    def unpack(src, carry):
        spread = jnp.broadcast_to(wbuf[src], (8, 128))
        for half in range(2):
            taken = jnp.take_along_axis(spread, where_word[half], axis=1)
            flag = jnp.bitwise_and(jnp.right_shift(taken, bit), 1).astype(jnp.float32)
            clear[src, 8 * half : 8 * half + 8, :] = flag
        return carry

    lax.fori_loop(0, NDEV, unpack, 0, unroll=8)

    def dates_of(first, rows):
        row = lax.broadcasted_iota(jnp.int32, (rows, 256), 0)
        return 4 * first + 4 * lax.div(row, 8) + lax.rem(row, 4)

    length = hl[0]
    weight = jnp.where(dates_of(0, 512) < length, both(clear, 0, 64), 0.0)
    weight16 = weight.astype(jnp.bfloat16)
    normal = jnp.zeros((288, 256), jnp.float32)
    for piece in range(3):
        normal = normal + jnp.dot(ln[piece], weight16, preferred_element_type=jnp.float32)
    lower = [[None] * COLS for _ in range(COLS)]
    index = 0
    for row in range(COLS):
        for col in range(row + 1):
            lower[row][col] = normal[8 * index : 8 * index + 8, :]
            index += 1
    count = lower[0][0]
    unit, inverse = factorise(lower)
    slot = 0
    for row in range(COLS):
        for col in range(row):
            usave[slot] = unit[row][col]
            slot += 1
    for row in range(COLS):
        usave[slot] = inverse[row]
        slot += 1
    usave[slot] = count

    pltpu.make_async_copy(v_h, inb, vrecv).wait()

    slot = 0
    unit = [[None] * COLS for _ in range(COLS)]
    for row in range(COLS):
        for col in range(row):
            unit[row][col] = usave[slot]
            slot += 1
    inverse = [usave[slot + row] for row in range(COLS)]
    count = usave[slot + COLS]

    seen = jnp.where(dates_of(0, 512) < length, both(clear, 0, 64), 0.0) * both(inb, 0, 64)
    target = jnp.dot(lt[...], seen, precision=lax.Precision.HIGHEST, preferred_element_type=jnp.float32)
    coeffs = substitute(unit, inverse, [target[8 * c : 8 * c + 8, :] for c in range(COLS)])
    place = lax.rem(lax.broadcasted_iota(jnp.int32, (8, 256), 0), 4)
    first, second = [], []
    for c in range(COLS):
        hi = coeffs[c].astype(jnp.bfloat16).astype(jnp.float32)
        mid = (coeffs[c] - hi).astype(jnp.bfloat16).astype(jnp.float32)
        lo = coeffs[c] - hi - mid
        first.append(jnp.where(place == 1, mid, jnp.where(place == 2, lo, hi)))
        second.append(jnp.where(place == 0, hi, jnp.where(place == 1, mid, 0.0)))
    stacked = jnp.concatenate(first + second, axis=0).astype(jnp.bfloat16)

    squares = jnp.zeros((8, 256), jnp.float32)
    for block in range(8):
        fitted = jnp.dot(fm[128 * block : 128 * block + 128, :], stacked, preferred_element_type=jnp.float32)
        left = both(clear, 16 * block, 16) * (both(inb, 16 * block, 16) - fitted)
        if block < 4:
            held = jnp.where(dates_of(16 * block, 128) < length, left * left, 0.0)
            squares = squares + jnp.sum(held.reshape(16, 8, 256), axis=0)
        if block >= 3:
            for piece, part in enumerate(split3(left)):
                resid[piece, 128 * (block - 3) : 128 * (block - 2), :] = part

    def rolled(x, shift):
        return pltpu.roll(x, shift, x.ndim - 2)

    odd = lax.rem(place, 2) == 1
    high = place >= 2

    def paired(x, combine, odd, high):
        x = combine(x, jnp.where(odd, rolled(x, 1), rolled(x, 7)))
        return combine(x, jnp.where(high, rolled(x, 2), rolled(x, 6)))

    squares = paired(squares, jnp.add, odd, high)
    sigma = jnp.sqrt(squares / (count - COLS) + 1e-06)
    scale = 1.0 / (sigma * jnp.sqrt(count))

    peak = jnp.zeros((8, 128), jnp.float32)
    big = jnp.broadcast_to(odd[None], (16, 8, 256)), jnp.broadcast_to(high[None], (16, 8, 256))
    for block in range(4):
        moving = jnp.zeros((128, 256), jnp.float32)
        for piece in range(3):
            moving = moving + jnp.dot(
                bm[...], resid[piece, 128 * block : 128 * block + 256, :], preferred_element_type=jnp.float32
            )
        level = invb[128 * block : 128 * block + 128, :]
        level = jnp.concatenate([level, level], axis=1).reshape(16, 8, 256)
        ratio = moving.reshape(16, 8, 256) * scale[None] * level
        ob[16 * block : 16 * block + 16, 0:8, :] = ratio[:, :, :128]
        ob[16 * block : 16 * block + 16, 8:16, :] = ratio[:, :, 128:]
        top = paired(jnp.abs(ratio), jnp.maximum, *big)
        turned = rolled(top, 4)
        spot = lax.broadcasted_iota(jnp.int32, (16, 8, 128), 1)
        rows = jnp.where(
            spot == 0,
            top[:, :, :128],
            jnp.where(spot == 1, turned[:, :, :128], jnp.where(spot == 2, top[:, :, 128:], turned[:, :, 128:])),
        )
        for step in range(16):
            ebuf[16 * block + step] = peak[0:4, :]
            peak = jnp.maximum(peak, rows[step])

    def deliver(step, local):
        other = lax.rem(me + step, 64)
        if local:
            pltpu.make_async_copy(ob.at[other], rb.at[me], rrecv).start()
            pltpu.make_async_copy(ebuf.at[other], eb.at[me], erecv).start()
            return
        to = device(other + 64)
        pltpu.make_async_remote_copy(
            ob.at[other], rb.at[me], rsend, rrecv, device_id=to, device_id_type=MESH
        ).start()
        pltpu.make_async_remote_copy(
            ebuf.at[other], eb.at[me], esend, erecv, device_id=to, device_id_type=MESH
        ).start()

    @pl.when(me < 64)
    def _():
        deliver(0, False)

    @pl.when(me >= 64)
    def _():
        deliver(0, True)

    for step in order(64, 2):
        deliver(step, False)

    pltpu.make_async_copy(wmsg.at[rest], wbuf.at[rest], wsend).wait()
    pltpu.make_async_copy(v_h.at[rest], inb.at[rest], vsend).wait()

    few = pl.ds(0, 63)
    one = pl.ds(0, 1)
    pltpu.make_async_copy(ob.at[few], rb.at[few], rsend).wait()
    pltpu.make_async_copy(ebuf.at[few], eb.at[few], esend).wait()

    @pl.when(me < 64)
    def _():
        pltpu.make_async_copy(ob.at[one], rb.at[one], rsend).wait()
        pltpu.make_async_copy(ebuf.at[one], eb.at[one], esend).wait()

    @pl.when(me >= 64)
    def _():
        pltpu.make_async_copy(inb, rb, rrecv).wait()
        pltpu.make_async_copy(eb, eb, erecv).wait()


def finish_kernel(rb, eb, ratio_out, peak_out):
    me = lax.axis_index("wide") * 4 + lax.axis_index("narrow")
    live = jnp.broadcast_to(me, (8, 128)) >= 64
    sub = lax.broadcasted_iota(jnp.int32, (8, 128), 0)
    date = lax.rem(sub, 4)
    for src in range(rb.shape[0]):
        for half in range(2):
            x = rb[src, 8 * half : 8 * half + 8, :]
            lower = jnp.broadcast_to(eb[src, 2 * half : 2 * half + 1, :], (8, 128))
            upper = jnp.broadcast_to(eb[src, 2 * half + 1 : 2 * half + 2, :], (8, 128))
            base = jnp.where(sub < 4, lower, upper)
            y = jnp.abs(x)
            y = jnp.maximum(y, jnp.where(date >= 1, pltpu.roll(y, 1, 0), 0.0))
            y = jnp.maximum(y, jnp.where(date >= 2, pltpu.roll(y, 2, 0), 0.0))
            y = jnp.maximum(y, base)
            ratio_out[src, 8 * half : 8 * half + 8, :] = jnp.where(live, x, 0.0)
            peak_out[src, 8 * half : 8 * half + 8, :] = jnp.where(live, y, 0.0)


def per_device(values, cloud_words, history_len, monitor_start, boundary_table):
    lhs_n, lhs_t, fit, band = constants()
    blocks = values.reshape(4, NDEV, 4, 128).transpose(1, 2, 0, 3).reshape(NDEV, 16, 128)
    f32, i32, bf16 = jnp.float32, jnp.int32, jnp.bfloat16
    dma = pltpu.SemaphoreType.DMA
    rb, eb = pl.pallas_call(
        fit_kernel,
        name="fit_exchange",
        out_shape=(jax.ShapeDtypeStruct((NDEV, 16, 128), f32), jax.ShapeDtypeStruct((NDEV, 4, 128), f32)),
        in_specs=[ANY] * 9,
        out_specs=(ANY, ANY),
        scratch_shapes=[
            pltpu.SMEM((1,), i32), pltpu.SMEM((1,), i32), pltpu.VMEM((4, 128), i32),
            pltpu.VMEM((4, 2048), i32), pltpu.VMEM((NDEV, 1, 128), i32), pltpu.VMEM((NDEV, 1, 128), i32),
            pltpu.VMEM((NDEV, 16, 128), f32), pltpu.VMEM((NDEV, 16, 128), f32),
            pltpu.VMEM((3, 640, 256), bf16), pltpu.VMEM((64, 16, 128), f32), pltpu.VMEM((64, 4, 128), f32),
            pltpu.VMEM(lhs_n.shape, bf16), pltpu.VMEM(lhs_t.shape, f32), pltpu.VMEM(fit.shape, bf16),
            pltpu.VMEM(band.shape, bf16), pltpu.VMEM((512, 128), f32), pltpu.VMEM((37, 8, 256), f32),
            dma((8,)), dma, dma, dma, dma, dma, dma, dma, dma,
        ],
        compiler_params=pltpu.CompilerParams(collective_id=0, has_side_effects=True, vmem_limit_bytes=40 << 20),
    )(
        history_len, monitor_start, boundary_table.reshape(4, 128), cloud_words, blocks,
        jnp.asarray(lhs_n), jnp.asarray(lhs_t), jnp.asarray(fit), jnp.asarray(band),
    )
    step = 16
    spec = pl.BlockSpec((step, 16, 128), lambda i: (i, 0, 0))
    ratio, peak = pl.pallas_call(
        finish_kernel,
        name="finish",
        grid=(NDEV // step,),
        out_shape=(jax.ShapeDtypeStruct((NDEV, 16, 128), f32),) * 2,
        in_specs=[spec, pl.BlockSpec((step, 4, 128), lambda i: (i, 0, 0))],
        out_specs=(spec, spec),
    )(rb, eb)

    def back(x):
        return x.reshape(NDEV, 4, 4, 128).transpose(2, 0, 1, 3).reshape(4, NDEV * 512)

    return back(ratio), back(peak)


def solution(mesh):
    placed = (P(("wide", "narrow"), None), P(("wide", "narrow"), None), P(), P(), P())
    return jax.shard_map(
        per_device,
        mesh=mesh,
        in_specs=placed,
        out_specs=(P(("wide", "narrow"), None), P(("wide", "narrow"), None)),
        check_vma=False,
    )
```

time: 98.9 us -> 57.1 us (0.58)
  the two profiles are of different devices: /device:TPU:1 before, /device:TPU:64 now
where the time goes in v1:
time: 57.1 us; the launch traced here: 56.1 us
  Pallas kernels  46 us (81%)
  local copies, waits for them, and re-layouts  8.19 us (14%)
  between operations  1.95 us (3%)
    pallas_call x1, Pallas kernels, per_device(): pl.pallas_call(fit_kernel, name='fit_exchange', out_shape=(jax.ShapeDtype...  40.5 us
    unnamed x18, local copies, waits for them, and re-layouts  8.19 us
    pallas_call x1, Pallas kernels, per_device(): pl.pallas_call(finish_kernel, name='finish', grid=(NDEV // step,), out_sh...  5.54 us

profile of v1, /device:TPU:64, one launch (start us, length us, event | category | flops | bytes accessed | tf_op | source)
XLA Modules:
  0.0 56.1 jit_solution(15084794723899250688)
XLA Ops:
  1.9 0.0 copy-start.8
  1.9 0.7 %copy-done.8 = s32[512]{0:T(512)S(1)} copy-done((s32[512]{0:T(512)S(1)}, s32[512]{0:T(512)}, u32[]{:S(2)}) %copy-start.8) | copy-done | bytes 2072
  2.6 0.0 copy-start
  2.6 1.2 %copy-done = f32[4,65536]{1,0:T(4,128)S(1)} copy-done((f32[4,65536]{1,0:T(4,128)S(1)}, f32[4,65536]{1,0:T(4,128)}, u32[]{:S(2)}) %copy-start) | copy-done | bytes 1048600
  3.8 0.0 copy-start.2
  3.8 1.2 %copy-done.2 = bf16[3,288,512]{2,1,0:T(8,128)(2,1)S(1)} copy-done((bf16[3,288,512]{2,1,0:T(8,128)(2,1)S(1)}, bf16[3,288,512]{2,1,0:T(8,128)(2,1)}, u32[]{:S(2)}) %copy-start.2) | copy-done | bytes 884760
  5.0 0.0 copy-start.4
  5.0 0.9 %copy-done.4 = bf16[1024,128]{1,0:T(8,128)(2,1)S(1)} copy-done((bf16[1024,128]{1,0:T(8,128)(2,1)S(1)}, bf16[1024,128]{1,0:T(8,128)(2,1)}, u32[]{:S(2)}) %copy-start.4) | copy-done | bytes 262168
  5.9 0.0 copy-start.5
  6.0 0.9 %copy-done.5 = f32[64,512]{1,0:T(8,128)S(1)} copy-done((f32[64,512]{1,0:T(8,128)S(1)}, f32[64,512]{1,0:T(8,128)}, u32[]{:S(2)}) %copy-start.5) | copy-done | bytes 131096
  6.9 0.0 copy-start.6
  6.9 0.8 %copy-done.6 = bf16[128,256]{1,0:T(8,128)(2,1)S(1)} copy-done((bf16[128,256]{1,0:T(8,128)(2,1)S(1)}, bf16[128,256]{1,0:T(8,128)(2,1)}, u32[]{:S(2)}) %copy-start.6) | copy-done | bytes 65560
  7.7 0.0 copy-start.7
  7.7 0.8 %copy-done.7 = s32[4,2048]{1,0:T(4,128)S(1)} copy-done((s32[4,2048]{1,0:T(4,128)S(1)}, s32[4,2048]{1,0:T(4,128)}, u32[]{:S(2)}) %copy-start.7) | copy-done | bytes 32792
  8.5 40.5 %fit_exchange.1 = (f32[128,16,128]{2,1,0:T(8,128)S(1)}, f32[128,4,128]{2,1,0:T(4,128)S(1)}) custom-call(s32[1]{0:T(128)S(6)} %copy.14.hl_h, s32[1]{0:T(128)S(6)} %copy.15.ms_h, s32[4,128]{1,0:T(4,128)S(1)} %bitcast.17, s32[4,2048]{1,0:T(4,128)S(1)} %copy-done.7, f32[128,16,128]{2,1,0:T(8,128)S(1)} %bitcast.16, bf16[3,288,512]{2,1,0:T(8,128)(2,1)S(1)} %copy-done.2, ...), custom_call_target="tpu_custom_call" | custom-call | tf_op jit(solution)/shard_map/fit_exchange/pallas_call | solution.py:373
  48.9 0.0 copy-start.1
  48.9 1.0 %copy-done.1 = f32[128,16,128]{2,1,0:T(8,128)} copy-done((f32[128,16,128]{2,1,0:T(8,128)}, f32[128,16,128]{2,1,0:T(8,128)S(1)}, u32[]{:S(2)}) %copy-start.1) | copy-done | bytes 1048600
  49.9 0.0 copy-start.3
  49.9 0.7 %copy-done.3 = f32[128,4,128]{2,1,0:T(4,128)} copy-done((f32[128,4,128]{2,1,0:T(4,128)}, f32[128,4,128]{2,1,0:T(4,128)S(1)}, u32[]{:S(2)}) %copy-start.3) | copy-done | bytes 262168
  50.6 5.5 %finish.1 = (f32[128,16,128]{2,1,0:T(8,128)}, f32[128,16,128]{2,1,0:T(8,128)}) custom-call(f32[128,16,128]{2,1,0:T(8,128)} %copy-done.1, f32[128,4,128]{2,1,0:T(4,128)} %copy-done.3), custom_call_target="tpu_custom_call" | custom-call | tf_op jit(solution)/shard_map/finish/pallas_call | solution.py:395
Async XLA Ops:
  1.9 0.7 %copy-start.8 = (s32[512]{0:T(512)S(1)}, s32[512]{0:T(512)}, u32[]{:S(2)}) copy-start(s32[512]{0:T(512)} %param.13) | copy-start | bytes 6148
  2.6 1.2 %copy-start = (f32[4,65536]{1,0:T(4,128)S(1)}, f32[4,65536]{1,0:T(4,128)}, u32[]{:S(2)}) copy-start(f32[4,65536]{1,0:T(4,128)} %param.9) | copy-start | bytes 3145732
  3.8 1.2 %copy-start.2 = (bf16[3,288,512]{2,1,0:T(8,128)(2,1)S(1)}, bf16[3,288,512]{2,1,0:T(8,128)(2,1)}, u32[]{:S(2)}) copy-start(bf16[3,288,512]{2,1,0:T(8,128)(2,1)} %constant.8.clone.ln_h) | copy-start | bytes 2654212
  5.0 0.9 %copy-start.4 = (bf16[1024,128]{1,0:T(8,128)(2,1)S(1)}, bf16[1024,128]{1,0:T(8,128)(2,1)}, u32[]{:S(2)}) copy-start(bf16[1024,128]{1,0:T(8,128)(2,1)} %constant.10.clone.fm_h) | copy-start | bytes 786436
  5.9 0.9 %copy-start.5 = (f32[64,512]{1,0:T(8,128)S(1)}, f32[64,512]{1,0:T(8,128)}, u32[]{:S(2)}) copy-start(f32[64,512]{1,0:T(8,128)} %constant.9.clone.lt_h) | copy-start | bytes 393220
  6.9 0.8 %copy-start.6 = (bf16[128,256]{1,0:T(8,128)(2,1)S(1)}, bf16[128,256]{1,0:T(8,128)(2,1)}, u32[]{:S(2)}) copy-start(bf16[128,256]{1,0:T(8,128)(2,1)} %constant.11.clone.bm_h) | copy-start | bytes 196612
  7.7 0.8 %copy-start.7 = (s32[4,2048]{1,0:T(4,128)S(1)}, s32[4,2048]{1,0:T(4,128)}, u32[]{:S(2)}) copy-start(s32[4,2048]{1,0:T(4,128)} %w_h.1) | copy-start | bytes 98308
  48.9 1.0 %copy-start.1 = (f32[128,16,128]{2,1,0:T(8,128)}, f32[128,16,128]{2,1,0:T(8,128)S(1)}, u32[]{:S(2)}) copy-start(f32[128,16,128]{2,1,0:T(8,128)S(1)} %get-tuple-element.6.rb) | copy-start | bytes 3145732
  49.9 0.7 %copy-start.3 = (f32[128,4,128]{2,1,0:T(4,128)}, f32[128,4,128]{2,1,0:T(4,128)S(1)}, u32[]{:S(2)}) copy-start(f32[128,4,128]{2,1,0:T(4,128)S(1)} %get-tuple-element.7.eb) | copy-start | bytes 786436

commit v2 on v1

--- a/solution.py
+++ b/solution.py
@@ -14,10 +14,14 @@
 HARMONICS = 3
 COLS = 8
 WINDOW = 64
+PARTS = 4
 DATES = 512
 NDEV = 128
 MESH = pl.DeviceIdType.MESH
+FULL_VMEM = 67043328
 ANY = pl.BlockSpec(memory_space=pl.ANY)
+HBM = pl.BlockSpec(memory_space=pltpu.HBM)
+VMEM = pl.BlockSpec(memory_space=pltpu.VMEM)
 
 
 def pieces(array, count=3):
@@ -346,23 +350,51 @@
         pltpu.make_async_copy(eb, eb, erecv).wait()
 
 
-def finish_kernel(rb, eb, ratio_out, peak_out):
+def finish_kernel(rb_h, eb_h, ratio_out, peak_out, rb, eb, peak, sem):
     me = lax.axis_index("wide") * 4 + lax.axis_index("narrow")
-    live = jnp.broadcast_to(me, (8, 128)) >= 64
+    group = NDEV // PARTS
     sub = lax.broadcasted_iota(jnp.int32, (8, 128), 0)
     date = lax.rem(sub, 4)
-    for src in range(rb.shape[0]):
-        for half in range(2):
-            x = rb[src, 8 * half : 8 * half + 8, :]
-            lower = jnp.broadcast_to(eb[src, 2 * half : 2 * half + 1, :], (8, 128))
-            upper = jnp.broadcast_to(eb[src, 2 * half + 1 : 2 * half + 2, :], (8, 128))
-            base = jnp.where(sub < 4, lower, upper)
-            y = jnp.abs(x)
-            y = jnp.maximum(y, jnp.where(date >= 1, pltpu.roll(y, 1, 0), 0.0))
-            y = jnp.maximum(y, jnp.where(date >= 2, pltpu.roll(y, 2, 0), 0.0))
-            y = jnp.maximum(y, base)
-            ratio_out[src, 8 * half : 8 * half + 8, :] = jnp.where(live, x, 0.0)
-            peak_out[src, 8 * half : 8 * half + 8, :] = jnp.where(live, y, 0.0)
+    loads, stores = [], []
+    for part in range(PARTS):
+        rows = pl.ds(group * part, group)
+        loads.append(
+            (
+                pltpu.make_async_copy(eb_h.at[rows], eb.at[rows], sem.at[4 * part]),
+                pltpu.make_async_copy(rb_h.at[rows], rb.at[rows], sem.at[4 * part + 1]),
+            )
+        )
+        for load in loads[-1]:
+            load.start()
+    for part in range(PARTS):
+        rows = pl.ds(group * part, group)
+        for load in loads[part]:
+            load.wait()
+
+        @pl.when(me < 64)
+        def _():
+            rb[rows] = jnp.zeros((group, 16, 128), jnp.float32)
+            eb[rows] = jnp.zeros((group, 4, 128), jnp.float32)
+
+        stores.append(pltpu.make_async_copy(rb.at[rows], ratio_out.at[rows], sem.at[4 * part + 2]))
+        stores[-1].start()
+
+        def one(step, carry):
+            src = group * part + step
+            for half in range(2):
+                y = jnp.abs(rb[src, 8 * half : 8 * half + 8, :])
+                lower = jnp.broadcast_to(eb[src, 2 * half : 2 * half + 1, :], (8, 128))
+                upper = jnp.broadcast_to(eb[src, 2 * half + 1 : 2 * half + 2, :], (8, 128))
+                y = jnp.maximum(y, jnp.where(date >= 1, pltpu.roll(y, 1, 0), 0.0))
+                y = jnp.maximum(y, jnp.where(date >= 2, pltpu.roll(y, 2, 0), 0.0))
+                peak[src, 8 * half : 8 * half + 8, :] = jnp.maximum(y, jnp.where(sub < 4, lower, upper))
+            return carry
+
+        lax.fori_loop(0, group, one, 0, unroll=8)
+        stores.append(pltpu.make_async_copy(peak.at[rows], peak_out.at[rows], sem.at[4 * part + 3]))
+        stores[-1].start()
+    for store in stores:
+        store.wait()
 
 
 def per_device(values, cloud_words, history_len, monitor_start, boundary_table):
@@ -374,7 +406,7 @@
         fit_kernel,
         name="fit_exchange",
         out_shape=(jax.ShapeDtypeStruct((NDEV, 16, 128), f32), jax.ShapeDtypeStruct((NDEV, 4, 128), f32)),
-        in_specs=[ANY] * 9,
+        in_specs=[HBM] * 9,
         out_specs=(ANY, ANY),
         scratch_shapes=[
             pltpu.SMEM((1,), i32), pltpu.SMEM((1,), i32), pltpu.VMEM((4, 128), i32),
@@ -385,20 +417,22 @@
             pltpu.VMEM(band.shape, bf16), pltpu.VMEM((512, 128), f32), pltpu.VMEM((37, 8, 256), f32),
             dma((8,)), dma, dma, dma, dma, dma, dma, dma, dma,
         ],
-        compiler_params=pltpu.CompilerParams(collective_id=0, has_side_effects=True, vmem_limit_bytes=40 << 20),
+        compiler_params=pltpu.CompilerParams(collective_id=0, has_side_effects=True, vmem_limit_bytes=FULL_VMEM),
     )(
         history_len, monitor_start, boundary_table.reshape(4, 128), cloud_words, blocks,
         jnp.asarray(lhs_n), jnp.asarray(lhs_t), jnp.asarray(fit), jnp.asarray(band),
     )
-    step = 16
-    spec = pl.BlockSpec((step, 16, 128), lambda i: (i, 0, 0))
     ratio, peak = pl.pallas_call(
         finish_kernel,
         name="finish",
-        grid=(NDEV // step,),
         out_shape=(jax.ShapeDtypeStruct((NDEV, 16, 128), f32),) * 2,
-        in_specs=[spec, pl.BlockSpec((step, 4, 128), lambda i: (i, 0, 0))],
-        out_specs=(spec, spec),
+        in_specs=[HBM, HBM],
+        out_specs=(HBM, HBM),
+        scratch_shapes=[
+            pltpu.VMEM((NDEV, 16, 128), f32), pltpu.VMEM((NDEV, 4, 128), f32), pltpu.VMEM((NDEV, 16, 128), f32),
+            dma((4 * PARTS,)),
+        ],
+        compiler_params=pltpu.CompilerParams(vmem_limit_bytes=FULL_VMEM),
     )(rb, eb)
 
     def back(x):

time: 57.1 us -> 46.1 us (0.81)
  local copies, waits for them, and re-layouts: 8.19 us -> 0 us
  Pallas kernels: 46 us -> 43.3 us
    unnamed x18 -> x0, local copies, waits for them, and re-layouts: 8.19 us -> none
    pallas_call x1, Pallas kernels: 5.54 us -> 2.45 us  [per_device(): pl.pallas_call(finish_kernel, name='finish', out_shape=(jax.ShapeDtypeStr...]
where the time goes in v2:
time: 46.1 us; the launch traced here: 45.2 us
  Pallas kernels  43.3 us (94%)
  between operations  1.93 us (4%)
    pallas_call x1, Pallas kernels, per_device(): pl.pallas_call(fit_kernel, name='fit_exchange', out_shape=(jax.ShapeDtype...  40.8 us
    pallas_call x1, Pallas kernels, per_device(): pl.pallas_call(finish_kernel, name='finish', out_shape=(jax.ShapeDtypeStr...  2.45 us

profile of v2, /device:TPU:64, one launch (start us, length us, event | category | flops | bytes accessed | tf_op | source)
XLA Modules:
  0.0 45.2 jit_solution(5664288249067722877)
XLA Ops:
  1.9 40.8 %fit_exchange.1 = (f32[128,16,128]{2,1,0:T(8,128)}, f32[128,4,128]{2,1,0:T(4,128)}) custom-call(s32[1]{0:T(128)S(6)} %copy.14.hl_h, s32[1]{0:T(128)S(6)} %copy.15.ms_h, s32[4,128]{1,0:T(4,128)} %bitcast.17, s32[4,2048]{1,0:T(4,128)} %w_h.1, f32[128,16,128]{2,1,0:T(8,128)} %bitcast.16, bf16[3,288,512]{2,1,0:T(8,128)(2,1)} %constant.8.clone.ln_h, ...), custom_call_target="tpu_custom_call" | custom-call | tf_op jit(solution)/shard_map/fit_exchange/pallas_call | solution.py:405
  42.7 2.4 %finish.1 = (f32[128,16,128]{2,1,0:T(8,128)}, f32[128,16,128]{2,1,0:T(8,128)}) custom-call(f32[128,16,128]{2,1,0:T(8,128)} %get-tuple-element.6.rb_h, f32[128,4,128]{2,1,0:T(4,128)} %get-tuple-element.7.eb_h), custom_call_target="tpu_custom_call" | custom-call | tf_op jit(solution)/shard_map/finish/pallas_call | solution.py:425

commit v3 on v2

v3 whole, which is shorter than its diff:
```python
import math
import random

import jax
import jax.numpy as jnp
import ml_dtypes
import numpy as np
from jax import lax
from jax.experimental import pallas as pl
from jax.experimental.pallas import tpu as pltpu
from jax.sharding import PartitionSpec as P

PERIOD = 46
HARMONICS = 3
COLS = 8
WINDOW = 64
PARTS = 4
DATES = 512
NDEV = 128
MESH = pl.DeviceIdType.MESH
FULL_VMEM = 67043328
ANY = pl.BlockSpec(memory_space=pl.ANY)
HBM = pl.BlockSpec(memory_space=pltpu.HBM)
VMEM = pl.BlockSpec(memory_space=pltpu.VMEM)


def pieces(array, count=3):
    out = []
    rest = array.astype(np.float64)
    for _ in range(count):
        part = rest.astype(np.float32).astype(ml_dtypes.bfloat16)
        out.append(part)
        rest = rest - part.astype(np.float64)
    return out


def constants():
    day = np.arange(DATES, dtype=np.float32)
    columns = [np.ones((DATES,), np.float32), day / np.float32(DATES)]
    for harmonic in range(1, HARMONICS + 1):
        phases = np.float32(2.0 * math.pi * harmonic / PERIOD) * day
        columns.append(np.cos(phases.astype(np.float64)).astype(np.float32))
        columns.append(np.sin(phases.astype(np.float64)).astype(np.float32))
    design = np.stack(columns, axis=1)
    row = np.arange(NDEV * 8)
    date = 4 * (row // 8) + row % 4
    parity = (row % 8) // 4
    sub = np.arange(8)
    hist = 512
    same = (sub[:, None] // 4 == parity[None, :hist]).astype(np.float64)
    outer = []
    for r in range(COLS):
        for c in range(r + 1):
            prod = (design[:, r] * design[:, c]).astype(np.float32)
            outer.append(same * prod[date[:hist]][None, :])
    lhs_n = np.stack(pieces(np.concatenate(outer, axis=0)), axis=0)
    lhs_t = np.concatenate([same * design[date[:hist], c][None, :] for c in range(COLS)], axis=0)
    lhs_t = lhs_t.astype(np.float32)
    d_hi, d_mid, d_lo = [p.astype(np.float64) for p in pieces(design)]
    fit = np.zeros((NDEV * 8, 128))
    for c in range(COLS):
        for p in range(2):
            on = parity == p
            col = 8 * c + 4 * p
            for slot, part in enumerate((d_hi, d_hi, d_hi, d_mid)):
                fit[:, col + slot] = on * part[date, c]
            for slot, part in enumerate((d_lo, d_mid)):
                fit[:, 64 + col + slot] = on * part[date, c]
    fit = fit.astype(ml_dtypes.bfloat16)
    lag = (date[:128][:, None] + 64) - date[:256][None, :]
    band = (lag >= 0) & (lag < WINDOW) & (parity[:128][:, None] == parity[:256][None, :])
    band = band.astype(ml_dtypes.bfloat16)
    return lhs_n, lhs_t, fit, band


def order(ranks, seed):
    ranks = list(ranks)
    random.Random(seed).shuffle(ranks)
    return ranks


def offsets(planes, axes):
    found = []
    for dz in range(planes):
        for dy in range(4):
            for dr in range(8):
                if (dz > 0) + (dy > 0) + (dr > 0) == axes:
                    found.append((dz, dy, dr))
    return found


def device(index):
    return {"wide": lax.div(index, 4), "narrow": lax.rem(index, 4)}


def split3(x):
    hi = x.astype(jnp.bfloat16)
    rest = x - hi.astype(jnp.float32)
    mid = rest.astype(jnp.bfloat16)
    lo = (rest - mid.astype(jnp.float32)).astype(jnp.bfloat16)
    return hi, mid, lo


def side(ref, half, start, count):
    return ref[start : start + count, 8 * half : 8 * half + 8, :].reshape(count * 8, 128)


def both(ref, start, count):
    return jnp.concatenate([side(ref, 0, start, count), side(ref, 1, start, count)], axis=1)


def factorise(lower):
    unit = [[None] * COLS for _ in range(COLS)]
    scaled = [[None] * COLS for _ in range(COLS)]
    inverse = []
    for col in range(COLS):
        for row in range(col, COLS):
            summed = lower[row][col]
            for mid in range(col):
                summed = summed - unit[row][mid] * scaled[col][mid]
            scaled[row][col] = summed
        inverse.append(1.0 / scaled[col][col])
        for row in range(col + 1, COLS):
            unit[row][col] = scaled[row][col] * inverse[col]
    return unit, inverse


def substitute(unit, inverse, target):
    forward = []
    for row in range(COLS):
        summed = target[row]
        for mid in range(row):
            summed = summed - unit[row][mid] * forward[mid]
        forward.append(summed)
    solved = [None] * COLS
    for row in reversed(range(COLS)):
        summed = forward[row] * inverse[row]
        for mid in range(row + 1, COLS):
            summed = summed - unit[mid][row] * solved[mid]
        solved[row] = summed
    return solved


def dates_of(first, rows, lanes):
    row = lax.broadcasted_iota(jnp.int32, (rows, lanes), 0)
    return 4 * first + 4 * lax.div(row, 8) + lax.rem(row, 4)


def rolled(x, shift):
    return pltpu.roll(x, shift, x.ndim - 2)


def over_dates(x, combine):
    place = lax.rem(lax.broadcasted_iota(jnp.int32, x.shape, x.ndim - 2), 4)
    x = combine(x, jnp.where(lax.rem(place, 2) == 1, rolled(x, 1), rolled(x, 7)))
    return combine(x, jnp.where(place >= 2, rolled(x, 2), rolled(x, 6)))


def fit_kernel(
    hl_h, ms_h, bt_h, w_h, v_h, ln_h, lt_h, fm_h, bm_h, rb, eb,
    hl, ms, bt, wv, wmsg, wbuf, inb, cb, clear, clearc, resid, ob, ebuf, mid, midb,
    ln, lt, fm, bm, invb, usave,
    csem, second, third, wsend, wrecv, vsend, vrecv, msend, mrecv, rsend, rrecv, esend, erecv,
):
    w = lax.axis_index("wide")
    narrow = lax.axis_index("narrow")
    me = w * 4 + narrow
    plane, column, place = lax.div(w, 8), lax.rem(lax.div(w, 2), 4), lax.rem(w, 2) * 4 + narrow
    lower, upper = me < 64, me >= 64
    barrier = pltpu.get_barrier_semaphore()

    def near(offset, flip=False):
        dz, dy, dr = offset
        z = plane
        if dz:
            z = 5 - plane if flip else lax.rem(plane + dz, 4)
        y = lax.rem(column + dy, 4) if dy else column
        r = lax.rem(place + dr, 8) if dr else place
        to = {"wide": z * 8 + y * 2 + lax.div(r, 4), "narrow": lax.rem(r, 4)}
        return z * 32 + y * 8 + r, (3 - z) * 32 + y * 8 + r, to

    def greet(sem, peers):
        for offset in peers:
            pl.semaphore_signal(sem, inc=1, device_id=near(offset)[2], device_id_type=MESH)

    one, two, three = offsets(4, 1), offsets(4, 2), offsets(4, 3)
    along_z = [offset for offset in one if offset[0]]
    along_y = [offset for offset in one if offset[1]]
    greet(barrier, one)
    loads = []
    for slot, (src, dst) in enumerate(
        ((w_h, wv), (hl_h, hl), (ms_h, ms), (bt_h, bt), (ln_h, ln), (lt_h, lt), (fm_h, fm), (bm_h, bm))
    ):
        loads.append(pltpu.make_async_copy(src, dst, csem.at[slot]))
        loads[-1].start()
    pltpu.make_async_copy(v_h.at[me, pl.ds(0, 8)], inb.at[me, pl.ds(0, 8)], vrecv.at[0]).start()
    pltpu.make_async_copy(v_h.at[me, pl.ds(8, 8)], inb.at[me, pl.ds(8, 8)], vrecv.at[1]).start()

    loads[0].wait()
    sub = lax.broadcasted_iota(jnp.int32, (8, 128), 0)
    lane = lax.broadcasted_iota(jnp.int32, (8, 128), 1)
    pick = 16 * sub + lax.rem(lane, 16)
    for tile in range(16):
        words = wv[:, 128 * tile : 128 * tile + 128]
        if tile >= 8:
            source = (3 - tile // 4) * 4 + tile % 4
            others = wv[:, 128 * source : 128 * source + 128]
        packed = jnp.zeros((8, 128), jnp.int32)
        for date in range(4):
            taken = jnp.take_along_axis(jnp.broadcast_to(words[date : date + 1, :], (8, 128)), pick, axis=1)
            if tile >= 8:
                extra = jnp.take_along_axis(jnp.broadcast_to(others[date : date + 1, :], (8, 128)), pick, axis=1)
                taken = jnp.where(lane < 64, taken, extra)
            packed = jnp.where(lax.div(lax.rem(lane, 64), 16) == date, taken, packed)
        wmsg[8 * tile : 8 * tile + 8] = packed.reshape(8, 1, 128)
    wbuf[pl.ds(me, 1)] = wmsg[pl.ds(me, 1)]

    def send(src, dst, sends, receives, to):
        pltpu.make_async_remote_copy(src, dst, sends, receives, device_id=to, device_id_type=MESH).start()

    def send_words(peers):
        for offset in peers:
            other, _, to = near(offset)
            send(wmsg.at[other], wbuf.at[me], wsend, wrecv, to)

    def send_half(half, peers):
        rows = pl.ds(8 * half, 8)
        for offset in peers:
            other, _, to = near(offset)
            send(v_h.at[other, rows], inb.at[me, rows], vsend, vrecv.at[half], to)

    def send_upper(peers):
        rows = pl.ds(8, 8)
        for offset in peers:
            other, partner, to = near(offset, True)
            send(v_h.at[other, rows], inb.at[me, rows], vsend, vrecv.at[1], to)
            send(v_h.at[partner, rows], cb.at[me - 64], vsend, vrecv.at[2], to)

    def send_second(axes):
        @pl.when(lower)
        def _():
            send_half(1, order(offsets(4, axes), axes))

        @pl.when(upper)
        def _():
            send_upper(order(offsets(2, axes), axes))

    mine = (3 - plane) * 32 + column * 8 + place

    @pl.when(upper)
    def _():
        pltpu.make_async_copy(v_h.at[mine, pl.ds(8, 8)], cb.at[me - 64], vrecv.at[2]).start()

    pl.semaphore_wait(barrier, len(one))
    greet(second, along_y + along_z)
    send_words(order(one, 1))
    send_second(1)
    pl.semaphore_wait(second, len(along_y + along_z))
    greet(third, along_z)
    send_words(order(two, 2))
    send_second(2)
    pl.semaphore_wait(third, len(along_z))
    send_words(order(three, 3))
    send_second(3)
    send_half(0, order(two + three, 4) + order(one, 5))

    for load in loads[1:]:
        load.wait()
    for part in range(2):
        date = 256 + 128 * part + lax.broadcasted_iota(jnp.int32, (1, 128), 1)
        line = 1.0 / (bt[2 + part : 3 + part, :].astype(jnp.float32) * 0.001)
        line = jnp.where(date >= ms[0], line, 0.0)
        rows = lax.broadcasted_iota(jnp.int32, (256, 128), 0)
        lanes = lax.broadcasted_iota(jnp.int32, (256, 128), 1)
        own = 4 * lax.div(rows, 8) + lax.rem(rows, 4)
        level = jnp.sum(jnp.where(lanes == own, line, 0.0), axis=1, keepdims=True)
        invb[256 * part : 256 * part + 256, :] = jnp.broadcast_to(level, (256, 128))

    rest = pl.ds(0, NDEV - 1)
    pltpu.make_async_copy(wmsg.at[rest], wbuf.at[rest], wrecv).wait()
    spots = [16 * lax.rem(sub, 4) + 4 * (2 * half + lax.div(sub, 4)) + lax.div(lane, 32) for half in range(2)]
    bit = lax.rem(lane, 32)

    def flags(src, spot):
        taken = jnp.take_along_axis(jnp.broadcast_to(wbuf[src], (8, 128)), spot, axis=1)
        return jnp.bitwise_and(jnp.right_shift(taken, bit), 1).astype(jnp.float32)

    def unpack(src, carry):
        for half in range(2):
            clear[src, 8 * half : 8 * half + 8, :] = flags(src, spots[half])
        return carry

    lax.fori_loop(0, NDEV, unpack, 0, unroll=8)

    length = hl[0]
    weight = jnp.where(dates_of(0, 512, 256) < length, both(clear, 0, 64), 0.0).astype(jnp.bfloat16)
    normal = jnp.zeros((288, 256), jnp.float32)
    for piece in range(3):
        normal = normal + jnp.dot(ln[piece], weight, preferred_element_type=jnp.float32)
    triangle = [[None] * COLS for _ in range(COLS)]
    index = 0
    for row in range(COLS):
        for col in range(row + 1):
            triangle[row][col] = normal[8 * index : 8 * index + 8, :]
            index += 1
    unit, inverse = factorise(triangle)
    saved = [unit[row][col] for row in range(COLS) for col in range(row)] + inverse + [triangle[0][0]]
    for slot, item in enumerate(saved):
        usave[slot] = item

    @pl.when(upper)
    def _():
        def unpack_upper(src, carry):
            clearc[src] = flags(64 + src, 64 + spots[1])
            return carry

        lax.fori_loop(0, 64, unpack_upper, 0, unroll=8)

    def stack(coeffs):
        lot = lax.rem(sub, 4)
        first, second = [], []
        for c in range(COLS):
            hi = coeffs[c].astype(jnp.bfloat16).astype(jnp.float32)
            middle = (coeffs[c] - hi).astype(jnp.bfloat16).astype(jnp.float32)
            lo = coeffs[c] - hi - middle
            first.append(jnp.where(lot == 1, middle, jnp.where(lot == 2, lo, hi)))
            second.append(jnp.where(lot == 0, hi, jnp.where(lot == 1, middle, 0.0)))
        return jnp.concatenate(first + second, axis=0).astype(jnp.bfloat16)

    def leftover(block, stacked, seen, shown):
        fitted = jnp.dot(fm[128 * block : 128 * block + 128, :], stacked, preferred_element_type=jnp.float32)
        return shown * (seen - fitted)

    def keep(block, left):
        for piece, part in enumerate(split3(left)):
            resid[piece, 128 * (block - 3) : 128 * (block - 2), :] = part

    def history(half):
        lanes = slice(128 * half, 128 * half + 128)
        unit = [[None] * COLS for _ in range(COLS)]
        slot = 0
        for row in range(COLS):
            for col in range(row):
                unit[row][col] = usave[slot, :, lanes]
                slot += 1
        inverse = [usave[slot + row, :, lanes] for row in range(COLS)]
        count = usave[slot + COLS, :, lanes]
        seen = jnp.where(dates_of(0, 512, 128) < length, side(clear, half, 0, 64), 0.0) * side(inb, half, 0, 64)
        target = jnp.dot(lt[...], seen, precision=lax.Precision.HIGHEST, preferred_element_type=jnp.float32)
        coeffs = substitute(unit, inverse, [target[8 * c : 8 * c + 8, :] for c in range(COLS)])
        stacked = stack(coeffs)
        squares = jnp.zeros((8, 128), jnp.float32)
        for block in range(4):
            left = leftover(block, stacked, side(inb, half, 16 * block, 16), side(clear, half, 16 * block, 16))
            held = jnp.where(dates_of(16 * block, 128, 128) < length, left * left, 0.0)
            squares = squares + jnp.sum(held.reshape(16, 8, 128), axis=0)
        squares = over_dates(squares, jnp.add)
        sigma = jnp.sqrt(squares / (count - COLS) + 1e-06)
        return coeffs, stacked, left, 1.0 / (sigma * jnp.sqrt(count))

    def monitor(slot, scale):
        peak = jnp.zeros((8, 128), jnp.float32)
        spot = lax.broadcasted_iota(jnp.int32, (16, 8, 128), 1)
        for block in range(4):
            moving = jnp.zeros((128, 128), jnp.float32)
            for piece in range(3):
                moving = moving + jnp.dot(
                    bm[...], resid[piece, 128 * block : 128 * block + 256, :], preferred_element_type=jnp.float32
                )
            level = invb[128 * block : 128 * block + 128, :].reshape(16, 8, 128)
            ratio = moving.reshape(16, 8, 128) * scale[None] * level
            ob[slot, 16 * block : 16 * block + 16] = ratio
            top = over_dates(jnp.abs(ratio), jnp.maximum)
            rows = jnp.where(spot == 0, top, rolled(top, 4))
            for step in range(16):
                ebuf[slot, 16 * block + step] = peak[0:2, :]
                peak = jnp.maximum(peak, rows[step])

    def deliver(slot, block, half, own):
        rows = pl.ds(8 * half, 8)
        for step in order(range(1, 64), 10 + slot):
            other = lax.rem(me + step, 64)
            to = device(other + 64)
            send(ob.at[slot, other], rb.at[block, rows], rsend, rrecv, to)
            send(ebuf.at[slot, other], eb.at[block, half], esend, erecv, to)
        other = lax.rem(me, 64)
        if own:
            pltpu.make_async_copy(ob.at[slot, other], rb.at[block, rows], rrecv).start()
            pltpu.make_async_copy(ebuf.at[slot, other], eb.at[block, half], erecv).start()
        else:
            to = device(other + 64)
            send(ob.at[slot, other], rb.at[block, rows], rsend, rrecv, to)
            send(ebuf.at[slot, other], eb.at[block, half], esend, erecv, to)

    first, all_rows, top_rows, low_rows = pl.ds(0, 64), pl.ds(0, NDEV), pl.ds(8, 8), pl.ds(0, 8)

    @pl.when(lower)
    def _():
        window = inb.at[first, top_rows]
        pltpu.make_async_copy(window, window, vrecv.at[1]).wait()
        coeffs, _, left, scale = history(1)
        mid[0:16] = left.reshape(16, 8, 128)
        for c in range(COLS):
            mid[16 + c] = coeffs[c]
        mid[24] = scale
        send(mid, midb, msend, mrecv, device(mine))

    @pl.when(upper)
    def _():
        window = inb.at[all_rows, top_rows]
        pltpu.make_async_copy(window, window, vrecv.at[1]).wait()
        _, stacked, left, scale = history(1)
        keep(3, left)
        for block in range(4, 8):
            keep(block, leftover(block, stacked, side(inb, 1, 16 * block, 16), side(clear, 1, 16 * block, 16)))
        monitor(0, scale)
        deliver(0, me, 1, True)

    window = inb.at[all_rows, low_rows]
    pltpu.make_async_copy(window, window, vrecv.at[0]).wait()
    _, stacked, left, scale = history(0)
    keep(3, left)
    for block in range(4, 8):
        keep(block, leftover(block, stacked, side(inb, 0, 16 * block, 16), side(clear, 0, 16 * block, 16)))
    monitor(1, scale)

    @pl.when(lower)
    def _():
        deliver(1, me, 0, False)

    @pl.when(upper)
    def _():
        deliver(1, me, 0, True)
        pltpu.make_async_copy(cb, cb, vrecv.at[2]).wait()
        pltpu.make_async_copy(midb, midb, mrecv).wait()
        stacked = stack([midb[16 + c] for c in range(COLS)])
        keep(3, midb[0:16].reshape(128, 128))
        for block in range(4, 8):
            start = 16 * block - 64
            keep(
                block,
                leftover(
                    block,
                    stacked,
                    cb[start : start + 16].reshape(128, 128),
                    clearc[start : start + 16].reshape(128, 128),
                ),
            )
        monitor(2, midb[24])
        deliver(2, mine, 1, True)

    pltpu.make_async_copy(wmsg.at[rest], wbuf.at[rest], wsend).wait()
    window = inb.at[rest, low_rows]
    pltpu.make_async_copy(window, window, vsend).wait()

    @pl.when(lower)
    def _():
        window = inb.at[rest, low_rows]
        pltpu.make_async_copy(window, window, vsend).wait()
        pltpu.make_async_copy(mid, mid, msend).wait()
        pltpu.make_async_copy(ob.at[1], ob.at[1], rsend).wait()
        pltpu.make_async_copy(ebuf.at[1], ebuf.at[1], esend).wait()

    @pl.when(upper)
    def _():
        window = inb.at[pl.ds(0, 126), low_rows]
        pltpu.make_async_copy(window, window, vsend).wait()
        for slot in range(3):
            few = ob.at[slot, pl.ds(0, 63)]
            pltpu.make_async_copy(few, few, rsend).wait()
            few = ebuf.at[slot, pl.ds(0, 63)]
            pltpu.make_async_copy(few, few, esend).wait()
        pltpu.make_async_copy(rb, rb, rrecv).wait()
        pltpu.make_async_copy(eb, eb, erecv).wait()


def finish_kernel(rb_h, eb_h, ratio_out, peak_out, rb, eb, peak, sem):
    me = lax.axis_index("wide") * 4 + lax.axis_index("narrow")
    group = NDEV // PARTS
    sub = lax.broadcasted_iota(jnp.int32, (8, 128), 0)
    date = lax.rem(sub, 4)
    loads, stores = [], []
    for part in range(PARTS):
        rows = pl.ds(group * part, group)
        loads.append(
            (
                pltpu.make_async_copy(eb_h.at[rows], eb.at[rows], sem.at[4 * part]),
                pltpu.make_async_copy(rb_h.at[rows], rb.at[rows], sem.at[4 * part + 1]),
            )
        )
        for load in loads[-1]:
            load.start()
    for part in range(PARTS):
        rows = pl.ds(group * part, group)
        for load in loads[part]:
            load.wait()

        @pl.when(me < 64)
        def _():
            rb[rows] = jnp.zeros((group, 16, 128), jnp.float32)
            eb[rows] = jnp.zeros((group, 2, 2, 128), jnp.float32)

        stores.append(pltpu.make_async_copy(rb.at[rows], ratio_out.at[rows], sem.at[4 * part + 2]))
        stores[-1].start()

        def one(step, carry):
            src = group * part + step
            for half in range(2):
                y = jnp.abs(rb[src, 8 * half : 8 * half + 8, :])
                lower = jnp.broadcast_to(eb[src, half, 0:1, :], (8, 128))
                upper = jnp.broadcast_to(eb[src, half, 1:2, :], (8, 128))
                y = jnp.maximum(y, jnp.where(date >= 1, pltpu.roll(y, 1, 0), 0.0))
                y = jnp.maximum(y, jnp.where(date >= 2, pltpu.roll(y, 2, 0), 0.0))
                peak[src, 8 * half : 8 * half + 8, :] = jnp.maximum(y, jnp.where(sub < 4, lower, upper))
            return carry

        lax.fori_loop(0, group, one, 0, unroll=8)
        stores.append(pltpu.make_async_copy(peak.at[rows], peak_out.at[rows], sem.at[4 * part + 3]))
        stores[-1].start()
    for store in stores:
        store.wait()


def per_device(values, cloud_words, history_len, monitor_start, boundary_table):
    lhs_n, lhs_t, fit, band = constants()
    blocks = values.reshape(4, NDEV, 4, 128).transpose(1, 2, 0, 3).reshape(NDEV, 16, 128)
    f32, i32, bf16 = jnp.float32, jnp.int32, jnp.bfloat16
    dma = pltpu.SemaphoreType.DMA
    rb, eb = pl.pallas_call(
        fit_kernel,
        name="fit_exchange",
        out_shape=(jax.ShapeDtypeStruct((NDEV, 16, 128), f32), jax.ShapeDtypeStruct((NDEV, 2, 2, 128), f32)),
        in_specs=[HBM] * 9,
        out_specs=(ANY, ANY),
        scratch_shapes=[
            pltpu.SMEM((1,), i32), pltpu.SMEM((1,), i32), pltpu.VMEM((4, 128), i32),
            pltpu.VMEM((4, 2048), i32), pltpu.VMEM((NDEV, 1, 128), i32), pltpu.VMEM((NDEV, 1, 128), i32),
            pltpu.VMEM((NDEV, 16, 128), f32), pltpu.VMEM((64, 8, 128), f32),
            pltpu.VMEM((NDEV, 16, 128), f32), pltpu.VMEM((64, 8, 128), f32),
            pltpu.VMEM((3, 640, 128), bf16), pltpu.VMEM((3, 64, 8, 128), f32), pltpu.VMEM((3, 64, 2, 128), f32),
            pltpu.VMEM((25, 8, 128), f32), pltpu.VMEM((25, 8, 128), f32),
            pltpu.VMEM(lhs_n.shape, bf16), pltpu.VMEM(lhs_t.shape, f32), pltpu.VMEM(fit.shape, bf16),
            pltpu.VMEM(band.shape, bf16), pltpu.VMEM((512, 128), f32), pltpu.VMEM((37, 8, 256), f32),
            dma((8,)), pltpu.SemaphoreType.REGULAR, pltpu.SemaphoreType.REGULAR,
            dma, dma, dma, dma((3,)), dma, dma, dma, dma, dma, dma,
        ],
        compiler_params=pltpu.CompilerParams(collective_id=0, has_side_effects=True, vmem_limit_bytes=FULL_VMEM),
    )(
        history_len, monitor_start, boundary_table.reshape(4, 128), cloud_words, blocks,
        jnp.asarray(lhs_n), jnp.asarray(lhs_t), jnp.asarray(fit), jnp.asarray(band),
    )
    ratio, peak = pl.pallas_call(
        finish_kernel,
        name="finish",
        out_shape=(jax.ShapeDtypeStruct((NDEV, 16, 128), f32),) * 2,
        in_specs=[HBM, HBM],
        out_specs=(HBM, HBM),
        scratch_shapes=[
            pltpu.VMEM((NDEV, 16, 128), f32), pltpu.VMEM((NDEV, 2, 2, 128), f32), pltpu.VMEM((NDEV, 16, 128), f32),
            dma((4 * PARTS,)),
        ],
        compiler_params=pltpu.CompilerParams(vmem_limit_bytes=FULL_VMEM),
    )(rb, eb)

    def back(x):
        return x.reshape(NDEV, 4, 4, 128).transpose(2, 0, 1, 3).reshape(4, NDEV * 512)

    return back(ratio), back(peak)


def solution(mesh):
    placed = (P(("wide", "narrow"), None), P(("wide", "narrow"), None), P(), P(), P())
    return jax.shard_map(
        per_device,
        mesh=mesh,
        in_specs=placed,
        out_specs=(P(("wide", "narrow"), None), P(("wide", "narrow"), None)),
        check_vma=False,
    )
```

time: 46.1 us -> 39.5 us (0.86); the launches traced: 45.2 us -> 39.3 us
  Pallas kernels: 43.3 us -> 37.4 us
    pallas_call x1, Pallas kernels: 40.8 us -> 34.9 us  [per_device(): pl.pallas_call(fit_kernel, name='fit_exchange', out_shape=(jax.ShapeDtype...]
where the time goes in v3:
time: 39.5 us; the launch traced here: 39.3 us
  Pallas kernels  37.4 us (95%)
  between operations  1.93 us (5%)
    pallas_call x1, Pallas kernels, per_device(): pl.pallas_call(fit_kernel, name='fit_exchange', out_shape=(jax.ShapeDtype...  34.9 us
    pallas_call x1, Pallas kernels, per_device(): pl.pallas_call(finish_kernel, name='finish', out_shape=(jax.ShapeDtypeStr...  2.45 us

profile of v3, /device:TPU:64, one launch (start us, length us, event | category | flops | bytes accessed | tf_op | source)
XLA Modules:
  0.0 39.3 jit_solution(9589961007768503984)
XLA Ops:
  1.9 34.9 %fit_exchange.1 = (f32[128,16,128]{2,1,0:T(8,128)}, f32[128,2,2,128]{3,2,1,0:T(2,128)}) custom-call(s32[1]{0:T(128)S(6)} %copy.14.hl_h, s32[1]{0:T(128)S(6)} %copy.15.ms_h, s32[4,128]{1,0:T(4,128)} %bitcast.17, s32[4,2048]{1,0:T(4,128)} %w_h.1, f32[128,16,128]{2,1,0:T(8,128)} %bitcast.16, bf16[3,288,512]{2,1,0:T(8,128)(2,1)} %constant.8.clone.ln_h, ...), custom_call_target="tpu_custom_call" | custom-call | tf_op jit(solution)/shard_map/fit_exchange/pallas_call | solution.py:529
  36.8 2.4 %finish.1 = (f32[128,16,128]{2,1,0:T(8,128)}, f32[128,16,128]{2,1,0:T(8,128)}) custom-call(f32[128,16,128]{2,1,0:T(8,128)} %get-tuple-element.6.rb_h, f32[128,2,2,128]{3,2,1,0:T(2,128)} %get-tuple-element.7.eb_h), custom_call_target="tpu_custom_call" | custom-call | tf_op jit(solution)/shard_map/finish/pallas_call | solution.py:552

commit v4 on v3

--- a/solution.py
+++ b/solution.py
@@ -378,19 +378,31 @@
 
     def deliver(slot, block, half, own):
         rows = pl.ds(8 * half, 8)
-        for step in order(range(1, 64), 10 + slot):
-            other = lax.rem(me + step, 64)
+
+        def far(other):
             to = device(other + 64)
             send(ob.at[slot, other], rb.at[block, rows], rsend, rrecv, to)
             send(ebuf.at[slot, other], eb.at[block, half], esend, erecv, to)
-        other = lax.rem(me, 64)
-        if own:
-            pltpu.make_async_copy(ob.at[slot, other], rb.at[block, rows], rrecv).start()
-            pltpu.make_async_copy(ebuf.at[slot, other], eb.at[block, half], erecv).start()
-        else:
-            to = device(other + 64)
-            send(ob.at[slot, other], rb.at[block, rows], rsend, rrecv, to)
-            send(ebuf.at[slot, other], eb.at[block, half], esend, erecv, to)
+
+        def post(other, check):
+            if not check:
+                far(other)
+                return
+
+            @pl.when(other + 64 == me)
+            def _():
+                pltpu.make_async_copy(ob.at[slot, other], rb.at[block, rows], rrecv).start()
+                pltpu.make_async_copy(ebuf.at[slot, other], eb.at[block, half], erecv).start()
+
+            @pl.when(other + 64 != me)
+            def _():
+                far(other)
+
+        base = lax.rem(column, 2) * 8 + place
+        for early in (0, 2, 1, 3):
+            for step in [0] + order(range(1, 16), 10 + slot):
+                other = (early // 2) * 32 + 16 * (early % 2) + lax.rem(base + step, 16)
+                post(other, step == 0 and own)
 
     first, all_rows, top_rows, low_rows = pl.ds(0, 64), pl.ds(0, NDEV), pl.ds(8, 8), pl.ds(0, 8)
 

time: 39.5 us -> 38.2 us (0.967)
  Pallas kernels: 37.4 us -> 35.8 us
    pallas_call x1, Pallas kernels: 34.9 us -> 33.4 us  [per_device(): pl.pallas_call(fit_kernel, name='fit_exchange', out_shape=(jax.ShapeDtype...]
where the time goes in v4:
time: 38.2 us; the launch traced here: 37.8 us
  Pallas kernels  35.8 us (94%)
  between operations  1.93 us (5%)
    pallas_call x1, Pallas kernels, per_device(): pl.pallas_call(fit_kernel, name='fit_exchange', out_shape=(jax.ShapeDtype...  33.4 us
    pallas_call x1, Pallas kernels, per_device(): pl.pallas_call(finish_kernel, name='finish', out_shape=(jax.ShapeDtypeStr...  2.45 us

profile of v4, /device:TPU:64, one launch (start us, length us, event | category | flops | bytes accessed | tf_op | source)
XLA Modules:
  0.0 37.8 jit_solution(11890340990165804500)
XLA Ops:
  1.9 33.4 %fit_exchange.1 = (f32[128,16,128]{2,1,0:T(8,128)}, f32[128,2,2,128]{3,2,1,0:T(2,128)}) custom-call(s32[1]{0:T(128)S(6)} %copy.14.hl_h, s32[1]{0:T(128)S(6)} %copy.15.ms_h, s32[4,128]{1,0:T(4,128)} %bitcast.17, s32[4,2048]{1,0:T(4,128)} %w_h.1, f32[128,16,128]{2,1,0:T(8,128)} %bitcast.16, bf16[3,288,512]{2,1,0:T(8,128)(2,1)} %constant.8.clone.ln_h, ...), custom_call_target="tpu_custom_call" | custom-call | tf_op jit(solution)/shard_map/fit_exchange/pallas_call | solution.py:541
  35.3 2.4 %finish.1 = (f32[128,16,128]{2,1,0:T(8,128)}, f32[128,16,128]{2,1,0:T(8,128)}) custom-call(f32[128,16,128]{2,1,0:T(8,128)} %get-tuple-element.6.rb_h, f32[128,2,2,128]{3,2,1,0:T(2,128)} %get-tuple-element.7.eb_h), custom_call_target="tpu_custom_call" | custom-call | tf_op jit(solution)/shard_map/finish/pallas_call | solution.py:564

commit v5 on v4

--- a/solution.py
+++ b/solution.py
@@ -255,6 +255,7 @@
     greet(second, along_y + along_z)
     send_words(order(one, 1))
     send_second(1)
+    send_half(0, order(one, 5))
     pl.semaphore_wait(second, len(along_y + along_z))
     greet(third, along_z)
     send_words(order(two, 2))
@@ -262,7 +263,7 @@
     pl.semaphore_wait(third, len(along_z))
     send_words(order(three, 3))
     send_second(3)
-    send_half(0, order(two + three, 4) + order(one, 5))
+    send_half(0, order(two + three, 4))
 
     for load in loads[1:]:
         load.wait()
@@ -400,7 +401,7 @@
 
         base = lax.rem(column, 2) * 8 + place
         for early in (0, 2, 1, 3):
-            for step in [0] + order(range(1, 16), 10 + slot):
+            for step in sorted([0] + order(range(1, 16), 10 + slot), key=lambda step: -(0, 1, 2, 1)[(step + 1) // 2 % 4]):
                 other = (early // 2) * 32 + 16 * (early % 2) + lax.rem(base + step, 16)
                 post(other, step == 0 and own)
 
@@ -412,9 +413,11 @@
         pltpu.make_async_copy(window, window, vrecv.at[1]).wait()
         coeffs, _, left, scale = history(1)
         mid[0:16] = left.reshape(16, 8, 128)
-        for c in range(COLS):
-            mid[16 + c] = coeffs[c]
-        mid[24] = scale
+        lot = lax.rem(sub, 4)
+        for part in range(2):
+            a, b, c, d = coeffs[4 * part : 4 * part + 4]
+            mid[16 + part] = jnp.where(lot == 0, a, jnp.where(lot == 1, b, jnp.where(lot == 2, c, d)))
+        mid[18] = scale
         send(mid, midb, msend, mrecv, device(mine))
 
     @pl.when(upper)
@@ -445,7 +448,9 @@
         deliver(1, me, 0, True)
         pltpu.make_async_copy(cb, cb, vrecv.at[2]).wait()
         pltpu.make_async_copy(midb, midb, mrecv).wait()
-        stacked = stack([midb[16 + c] for c in range(COLS)])
+        lot = lax.rem(sub, 4)
+        spread = [over_dates(jnp.where(lot == c % 4, midb[16 + c // 4], 0.0), jnp.add) for c in range(COLS)]
+        stacked = stack(spread)
         keep(3, midb[0:16].reshape(128, 128))
         for block in range(4, 8):
             start = 16 * block - 64
@@ -458,7 +463,7 @@
                     clearc[start : start + 16].reshape(128, 128),
                 ),
             )
-        monitor(2, midb[24])
+        monitor(2, midb[18])
         deliver(2, mine, 1, True)
 
     pltpu.make_async_copy(wmsg.at[rest], wbuf.at[rest], wsend).wait()
@@ -550,7 +555,7 @@
             pltpu.VMEM((NDEV, 16, 128), f32), pltpu.VMEM((64, 8, 128), f32),
             pltpu.VMEM((NDEV, 16, 128), f32), pltpu.VMEM((64, 8, 128), f32),
             pltpu.VMEM((3, 640, 128), bf16), pltpu.VMEM((3, 64, 8, 128), f32), pltpu.VMEM((3, 64, 2, 128), f32),
-            pltpu.VMEM((25, 8, 128), f32), pltpu.VMEM((25, 8, 128), f32),
+            pltpu.VMEM((19, 8, 128), f32), pltpu.VMEM((19, 8, 128), f32),
             pltpu.VMEM(lhs_n.shape, bf16), pltpu.VMEM(lhs_t.shape, f32), pltpu.VMEM(fit.shape, bf16),
             pltpu.VMEM(band.shape, bf16), pltpu.VMEM((512, 128), f32), pltpu.VMEM((37, 8, 256), f32),
             dma((8,)), pltpu.SemaphoreType.REGULAR, pltpu.SemaphoreType.REGULAR,

time: 38.2 us -> 38 us (level)
  no operation moved by 1% of the time
where the time goes in v5:
time: 38 us; the launch traced here: 37.8 us
  Pallas kernels  35.9 us (94%)
  between operations  1.93 us (5%)
    pallas_call x1, Pallas kernels, per_device(): pl.pallas_call(fit_kernel, name='fit_exchange', out_shape=(jax.ShapeDtype...  33.5 us
    pallas_call x1, Pallas kernels, per_device(): pl.pallas_call(finish_kernel, name='finish', out_shape=(jax.ShapeDtypeStr...  2.45 us

profile of v5, /device:TPU:64, one launch (start us, length us, event | category | flops | bytes accessed | tf_op | source)
XLA Modules:
  0.0 37.8 jit_solution(2724352193669474899)
XLA Ops:
  1.9 33.5 %fit_exchange.1 = (f32[128,16,128]{2,1,0:T(8,128)}, f32[128,2,2,128]{3,2,1,0:T(2,128)}) custom-call(s32[1]{0:T(128)S(6)} %copy.14.hl_h, s32[1]{0:T(128)S(6)} %copy.15.ms_h, s32[4,128]{1,0:T(4,128)} %bitcast.17, s32[4,2048]{1,0:T(4,128)} %w_h.1, f32[128,16,128]{2,1,0:T(8,128)} %bitcast.16, bf16[3,288,512]{2,1,0:T(8,128)(2,1)} %constant.8.clone.ln_h, ...), custom_call_target="tpu_custom_call" | custom-call | tf_op jit(solution)/shard_map/fit_exchange/pallas_call | solution.py:546
  35.4 2.4 %finish.1 = (f32[128,16,128]{2,1,0:T(8,128)}, f32[128,16,128]{2,1,0:T(8,128)}) custom-call(f32[128,16,128]{2,1,0:T(8,128)} %get-tuple-element.6.rb_h, f32[128,2,2,128]{3,2,1,0:T(2,128)} %get-tuple-element.7.eb_h), custom_call_target="tpu_custom_call" | custom-call | tf_op jit(solution)/shard_map/finish/pallas_call | solution.py:569

commit v6 on v5

--- a/solution.py
+++ b/solution.py
@@ -236,14 +236,17 @@
             send(v_h.at[other, rows], inb.at[me, rows], vsend, vrecv.at[1], to)
             send(v_h.at[partner, rows], cb.at[me - 64], vsend, vrecv.at[2], to)
 
-    def send_second(axes):
+    def send_second(axes, tilted=None):
+        def chosen(planes):
+            return [o for o in offsets(planes, axes) if tilted is None or (o[0] > 0) == bool(tilted)]
+
         @pl.when(lower)
         def _():
-            send_half(1, order(offsets(4, axes), axes))
+            send_half(1, order(chosen(4), axes))
 
         @pl.when(upper)
         def _():
-            send_upper(order(offsets(2, axes), axes))
+            send_upper(order(chosen(2), axes))
 
     mine = (3 - plane) * 32 + column * 8 + place
 
@@ -252,14 +255,19 @@
         pltpu.make_async_copy(v_h.at[mine, pl.ds(8, 8)], cb.at[me - 64], vrecv.at[2]).start()
 
     pl.semaphore_wait(barrier, len(one))
-    greet(second, along_y + along_z)
+    greet(second.at[0], along_y)
+    greet(second.at[1], along_z)
     send_words(order(one, 1))
     send_second(1)
     send_half(0, order(one, 5))
-    pl.semaphore_wait(second, len(along_y + along_z))
+    pl.semaphore_wait(second.at[0], len(along_y))
     greet(third, along_z)
-    send_words(order(two, 2))
-    send_second(2)
+    flat = [offset for offset in two if not offset[0]]
+    send_words(order(flat, 2))
+    send_second(2, 0)
+    pl.semaphore_wait(second.at[1], len(along_z))
+    send_words(order([offset for offset in two if offset[0]], 2))
+    send_second(2, 1)
     pl.semaphore_wait(third, len(along_z))
     send_words(order(three, 3))
     send_second(3)
@@ -558,7 +566,7 @@
             pltpu.VMEM((19, 8, 128), f32), pltpu.VMEM((19, 8, 128), f32),
             pltpu.VMEM(lhs_n.shape, bf16), pltpu.VMEM(lhs_t.shape, f32), pltpu.VMEM(fit.shape, bf16),
             pltpu.VMEM(band.shape, bf16), pltpu.VMEM((512, 128), f32), pltpu.VMEM((37, 8, 256), f32),
-            dma((8,)), pltpu.SemaphoreType.REGULAR, pltpu.SemaphoreType.REGULAR,
+            dma((8,)), pltpu.SemaphoreType.REGULAR((2,)), pltpu.SemaphoreType.REGULAR,
             dma, dma, dma, dma((3,)), dma, dma, dma, dma, dma, dma,
         ],
         compiler_params=pltpu.CompilerParams(collective_id=0, has_side_effects=True, vmem_limit_bytes=FULL_VMEM),

time: 38 us -> 37.9 us (level)
  no operation moved by 1% of the time
where the time goes in v6:
time: 37.9 us; the launch traced here: 37.7 us
  Pallas kernels  35.8 us (94%)
  between operations  1.93 us (5%)
    pallas_call x1, Pallas kernels, per_device(): pl.pallas_call(fit_kernel, name='fit_exchange', out_shape=(jax.ShapeDtype...  33.4 us
    pallas_call x1, Pallas kernels, per_device(): pl.pallas_call(finish_kernel, name='finish', out_shape=(jax.ShapeDtypeStr...  2.45 us

profile of v6, /device:TPU:64, one launch (start us, length us, event | category | flops | bytes accessed | tf_op | source)
XLA Modules:
  0.0 37.7 jit_solution(6277267841231831097)
XLA Ops:
  1.9 33.4 %fit_exchange.1 = (f32[128,16,128]{2,1,0:T(8,128)}, f32[128,2,2,128]{3,2,1,0:T(2,128)}) custom-call(s32[1]{0:T(128)S(6)} %copy.14.hl_h, s32[1]{0:T(128)S(6)} %copy.15.ms_h, s32[4,128]{1,0:T(4,128)} %bitcast.17, s32[4,2048]{1,0:T(4,128)} %w_h.1, f32[128,16,128]{2,1,0:T(8,128)} %bitcast.16, bf16[3,288,512]{2,1,0:T(8,128)(2,1)} %constant.8.clone.ln_h, ...), custom_call_target="tpu_custom_call" | custom-call | tf_op jit(solution)/shard_map/fit_exchange/pallas_call | solution.py:554
  35.3 2.4 %finish.1 = (f32[128,16,128]{2,1,0:T(8,128)}, f32[128,16,128]{2,1,0:T(8,128)}) custom-call(f32[128,16,128]{2,1,0:T(8,128)} %get-tuple-element.6.rb_h, f32[128,2,2,128]{3,2,1,0:T(2,128)} %get-tuple-element.7.eb_h), custom_call_target="tpu_custom_call" | custom-call | tf_op jit(solution)/shard_map/finish/pallas_call | solution.py:577
